TPU v7x, 32 devices: a whole 2x2x4 slice. The times are simulated.
32 devices in a mesh: groups: 2 (over y), sec: 4 (over z), blk: 4 (over x, core).
Axes of the slice: x: 2, y: 2, z: 4, core: 2. Of those that a mesh axis runs over, the one named last changes fastest.
Arguments:
- psi: bfloat16 [8, 4, 256, 256], P(('groups', 'sec'), 'blk'), parts along dimension 0, may hold values from -6 to 6
- own_env: bfloat16 [8, 4, 17, 256, 256], P(('groups', 'sec'), 'blk'), parts along dimension 0, may hold values from -0.375 to 0.375
- handoff_env: bfloat16 [8, 4, 17, 256, 256], P(('groups', 'sec'), 'blk'), parts along dimension 0, may hold values from -0.375 to 0.375
- sources: int32 [8, 4, 17], P(('groups', 'sec'), 'blk'), parts along dimension 0, may hold values from 0 to 3, as said below
Outputs:
- applied: bfloat16 [8, 4, 256, 256], P(('groups', 'sec'), 'blk'), parts along dimension 0
- rayleigh: float32 [8], P(('groups', 'sec')), parts along dimension 0
- residual_scale: float32 [8], P(('groups', 'sec')), parts along dimension 0
There are 2 independent parts, one for each index of `groups`. A program takes and returns all parts, laid end to end along the dimension named above; each array names one. Nothing has to cross between parts.
Inputs may be any that keep to these rules, and one draw needn't show every extreme that they name: `sources`: every entry names a sector of the same section, and the 17 channels of each output sector name every one of the 4 sectors of its section.
All inputs are finite; a program needn't handle non-finite values.
Results may differ from a plain program's by a relative error of at most 0.0064.
Values may be sent and summed in bfloat16 or wider, within the bound.
No kernel may reach another device: no remote copies, remote signals or barrier semaphores. Data moves between devices by JAX's collectives and lax.ppermute only.
A program may use at most 64 MiB of HBM per device.

v0:
```python
import functools

import jax
import jax.numpy as jnp
from jax import lax
from jax.experimental import pallas as pl
from jax.experimental.pallas import tpu as pltpu
from jax.sharding import PartitionSpec as P


f32 = jnp.float32
bf16 = jnp.bfloat16
EXTRA = 8
GROUP = 5

ANY = pl.BlockSpec(memory_space=pl.ANY)
HBM = pl.BlockSpec(memory_space=pltpu.HBM)
VMEM = pl.BlockSpec(memory_space=pltpu.VMEM)
SMEM = pl.BlockSpec(memory_space=pltpu.SMEM)
PARAMS = pltpu.CompilerParams(vmem_limit_bytes=16 * 1024 * 1024)


def swap(value, axis, bit):
    return lax.ppermute(value, axis, [(i, i ^ bit) for i in range(lax.axis_size(axis))])


def dot(a, b):
    return jnp.dot(a, b, preferred_element_type=f32)


def total_of(x):
    return jnp.sum(x, axis=(0, 1), keepdims=True)


def call(kernel, ins, outs, args, flops, aliases=None, scratch=()):
    return pl.pallas_call(
        kernel,
        in_specs=ins,
        out_specs=[spec for spec, _ in outs],
        out_shape=[shape for _, shape in outs],
        scratch_shapes=scratch,
        input_output_aliases=aliases or {},
        compiler_params=PARAMS,
        cost_estimate=pl.CostEstimate(flops=flops, transcendentals=0, bytes_accessed=0),
    )(*args)


def one_channel(table, psi, env, c):
    parity = table[0]
    source = table[2 + c]
    inner = dot(psi[source], env[1 - parity, c]).astype(bf16)
    return source, dot(env[parity, c], inner)


def cut_kernel(base, whole, *refs):
    pieces, sem = refs[:-1], refs[-1]
    copies = []
    for k, piece in enumerate(pieces):
        size = piece.shape[0]
        copies.append(pltpu.make_async_copy(whole.at[pl.ds(base, size)], piece, sem.at[k]))
        base += size
    for copy in copies:
        copy.start()
    for copy in copies:
        copy.wait()


def opening_kernel(table, psi, own, chunk, env, parts, mass, order, starts, kept, sem):
    copy = pltpu.make_async_copy(own, env.at[0], sem)
    copy.start()
    channels = own.shape[0]
    width = psi.shape[0]
    me = table[1]
    for k in range(table.shape[0]):
        kept[k] = table[k]
    for k in range(chunk.shape[0]):
        env[1, k] = chunk[k]
    parts[...] = jnp.zeros_like(parts)
    for s in range(width):
        wide = psi[s].astype(f32)
        mass[s] = jnp.broadcast_to(total_of(wide * wide), mass.shape[1:])

    def by_source(m, place):
        starts[m] = place

        def look(c, at):
            order[at] = c
            return at + (table[2 + c] ^ me == m).astype(jnp.int32)

        return lax.fori_loop(0, channels, look, place)

    starts[width] = lax.fori_loop(0, width, by_source, 0)
    copy.wait()
    for k in range(chunk.shape[0]):
        source, product = one_channel(table, psi, env, k)
        parts[source] += product


def middle_kernel(base, table, psi, chunk, env_in, parts_in, env, parts, early, along):
    for k in range(chunk.shape[0]):
        env[1, base + k] = chunk[k]
    for k in range(chunk.shape[0]):
        source, product = one_channel(table, psi, env, base + k)
        parts[source] += product
    total = parts[0]
    for s in range(1, parts.shape[0]):
        total = total + parts[s]
    early[...] = total
    along[...] = jnp.broadcast_to(total_of(psi[table[1]].astype(f32) * total), along.shape)


def closing_kernel(base, table, psi, chunk, env_in, parts_in, early, along, mass, env, parts, packed):
    me = table[1]
    first = early[...]
    for k in range(chunk.shape[0]):
        env[1, base + k] = chunk[k]
    late = None
    for k in range(chunk.shape[0]):
        source, product = one_channel(table, psi, env, base + k)
        parts[source] += product
        late = product if late is None else late + product
    wide = psi[me].astype(f32)
    along_all = along[:1, :1] + total_of(wide * late)
    weight = mass[me][:1, :1]
    share = jnp.where(weight > 0, along_all / jnp.where(weight > 0, weight, 1.0), 0.0)
    rows, columns = first.shape
    packed[:rows] = (first + late - share * wide).astype(bf16)
    high = share.astype(bf16).astype(f32)
    middle = (share - high).astype(bf16).astype(f32)
    low = share - high - middle
    row = lax.broadcasted_iota(jnp.int32, (EXTRA, columns), 0)
    tail = jnp.where(row == 0, high, jnp.where(row == 1, middle, jnp.where(row == 2, low, 0.0)))
    packed[rows:] = tail.astype(bf16)


def gathered(table, order, psi_rows, env, blocks, held, low, begin, end):
    parity, me = table[0], table[1]
    lefts, inners = [], []
    for k in range(GROUP):
        valid = begin + k < end
        c = order[jnp.where(valid, begin + k, 0)]
        if len(blocks) > 1:
            vector = held[jnp.where(valid, (table[2 + c] ^ me) - low, 0)]
        else:
            vector = blocks[0][:psi_rows]
        inner = dot(vector, env[1 - parity, c])
        inners.append(jnp.where(valid, inner, 0.0).astype(bf16))
        lefts.append(env[parity, c])
    return dot(jnp.concatenate(lefts, axis=1), jnp.concatenate(inners, axis=0))


def own_sums(block, psi):
    rows = psi.shape[0]
    bits = block[rows:].astype(f32)
    share = bits[0:1, 0:1] + bits[1:2, 0:1] + bits[2:3, 0:1]
    value = block[:rows].astype(f32)
    return share, total_of(value * value), total_of(value * psi[...].astype(f32))


def second_kernel(low, high, table, order, starts, psi, env, *refs):
    count = high - low
    blocks, refs = refs[:count], refs[count:]
    if low:
        before, refs = refs[0], refs[1:]
    summed, stats, held = refs
    me = table[1]
    rows, columns = psi.shape[1:]
    if count > 1:
        for k in range(count):
            held[k] = blocks[k][:rows]
    summed[...] = before[...] if low else jnp.zeros((rows, columns), f32)
    begin, end = starts[low], starts[high]

    def step(g, carry):
        summed[...] += gathered(table, order, rows, env, blocks, held, low, begin + g * GROUP, end)
        return carry

    lax.fori_loop(0, (end - begin + GROUP - 1) // GROUP, step, 0)
    for k in range(count):
        for j, value in enumerate(own_sums(blocks[k], psi.at[me ^ (low + k)])):
            stats[k, j] = jnp.broadcast_to(value, stats.shape[2:])


def final_kernel(low, more, table, order, starts, psi, env, block, before, mass, parts, *refs):
    stats_in, refs = refs[:more], refs[more:]
    applied, alpha_out, scale_out, summed, ready, alpha_held, scale_held, sem = refs
    me = table[1]
    width, rows, columns = parts.shape
    begin, end = starts[low], starts[width]
    summed[...] = before[...]

    def step(g, carry):
        summed[...] += gathered(table, order, rows, env, [block], None, low, begin + g * GROUP, end)
        return carry

    lax.fori_loop(1, (end - begin + GROUP - 1) // GROUP, step, 0)

    triples = []
    for ref in stats_in:
        for k in range(ref.shape[0]):
            triples.append(tuple(ref[k, j][:1, :1] for j in range(3)))
    triples.append(own_sums(block, psi.at[me ^ low]))
    along = jnp.zeros((1, 1), f32)
    whole = jnp.zeros((1, 1), f32)
    for m in range(width):
        weight = mass[me ^ m][:1, :1]
        along += triples[m][0] * weight
        whole += weight
    alpha = along / whole
    power = jnp.zeros((1, 1), f32)
    total = summed[...]
    for m in range(width):
        share, square, cross = triples[m]
        delta = share - alpha
        power += square + 2.0 * delta * cross + delta * delta * mass[me ^ m][:1, :1]
        total += delta * parts[me ^ m]
    scale = jnp.sqrt(power / (width * rows * columns) + 1e-06)
    alpha_held[0] = alpha[0, 0]
    scale_held[0] = scale[0, 0]
    copies = [
        pltpu.make_async_copy(alpha_held, alpha_out, sem.at[0]),
        pltpu.make_async_copy(scale_held, scale_out, sem.at[1]),
        pltpu.make_async_copy(ready, applied, sem.at[2]),
    ]
    copies[0].start()
    copies[1].start()
    total += gathered(table, order, rows, env, [block], None, low, begin, end)
    ready[...] = (total / scale).astype(bf16)
    copies[2].start()
    for copy in copies:
        copy.wait()


def chunk_sizes(channels):
    return [2, channels - 3, 1]


def shards(psi, own_env, handoff_env, sources):
    own, handoff = own_env[0, 0], handoff_env[0, 0]
    channels, block = own.shape[0], own.shape[1:]
    width = lax.axis_size("blk")
    work = 4 * block[0] ** 3
    sizes = chunk_sizes(channels)
    bases = [sum(sizes[:k]) for k in range(len(sizes))]
    handoff = pltpu.with_memory_space_constraint(handoff, pltpu.HBM)
    pieces = []
    for low, high in ((0, 1), (1, len(sizes))):
        pieces += call(
            functools.partial(cut_kernel, bases[low]),
            [HBM],
            [(VMEM, pltpu.VMEM((size,) + block, bf16)) for size in sizes[low:high]],
            (handoff,),
            0,
            scratch=[pltpu.SemaphoreType.DMA((high - low,))],
        )
    chunks = []
    for piece in pieces:
        chunks.append(swap(piece, "sec", 1))
    table = jnp.concatenate(
        [jnp.stack([lax.axis_index("sec") % 2, lax.axis_index("blk")]).astype(jnp.int32), sources[0, 0]]
    )
    psis = lax.all_gather(psi[0, 0], "blk", axis=0)

    env_shape = (VMEM, pltpu.VMEM((2, channels) + block, bf16))
    parts_shape = (VMEM, pltpu.VMEM((width,) + block, f32))
    tile = (8, 128)
    env, parts, mass, order, starts, table = call(
        opening_kernel,
        [SMEM, VMEM, HBM, VMEM],
        [
            env_shape,
            parts_shape,
            (VMEM, pltpu.VMEM((width,) + tile, f32)),
            (SMEM, pltpu.SMEM((channels + 1,), jnp.int32)),
            (SMEM, pltpu.SMEM((width + 1,), jnp.int32)),
            (SMEM, pltpu.SMEM(table.shape, jnp.int32)),
        ],
        (table, psis, pltpu.with_memory_space_constraint(own, pltpu.HBM), chunks[0]),
        work * sizes[0],
        scratch=[pltpu.SemaphoreType.DMA],
    )
    for k in range(1, len(sizes) - 1):
        env, parts, early, along = call(
            functools.partial(middle_kernel, bases[k]),
            [SMEM, VMEM, VMEM, VMEM, VMEM],
            [env_shape, parts_shape, (VMEM, pltpu.VMEM(block, f32)), (VMEM, pltpu.VMEM(tile, f32))],
            (table, psis, chunks[k], env, parts),
            work * sizes[k],
            aliases={3: 0, 4: 1},
        )
    env, parts, packed = call(
        functools.partial(closing_kernel, bases[-1]),
        [SMEM, VMEM, VMEM, VMEM, VMEM, VMEM, VMEM, VMEM],
        [env_shape, parts_shape, (VMEM, pltpu.VMEM((block[0] + EXTRA, block[1]), bf16))],
        (table, psis, chunks[-1], env, parts, early, along, mass),
        work * sizes[-1],
        aliases={3: 0, 4: 1},
    )

    blocks = {0: packed}
    bit = width // 2
    while bit:
        for m in sorted(blocks):
            blocks[m | bit] = swap(blocks[m], "blk", bit)
        bit //= 2

    cuts = sorted({0, min(2, width - 1), width - 1})
    shared = [table, order, starts, psis, env]
    shared_specs = [SMEM, SMEM, SMEM, VMEM, VMEM]
    summed, stats = None, []
    for low, high in zip(cuts[:-1], cuts[1:]):
        count = high - low
        args = shared + [blocks[m] for m in range(low, high)] + ([summed] if low else [])
        summed, stat = call(
            functools.partial(second_kernel, low, high),
            shared_specs + [VMEM] * (len(args) - len(shared)),
            [(VMEM, pltpu.VMEM(block, f32)), (VMEM, pltpu.VMEM((count, 3) + tile, f32))],
            tuple(args),
            work * channels * count // width,
            scratch=[pltpu.VMEM((count,) + block, bf16)],
        )
        stats.append(stat)
    args = shared + [blocks[width - 1], summed, mass, parts] + stats
    applied, alpha, scale = call(
        functools.partial(final_kernel, width - 1, len(stats)),
        shared_specs + [VMEM] * (len(args) - len(shared)),
        [
            (HBM, jax.ShapeDtypeStruct(block, bf16)),
            (HBM, jax.ShapeDtypeStruct((1,), f32)),
            (HBM, jax.ShapeDtypeStruct((1,), f32)),
        ],
        tuple(args),
        work * channels // width,
        scratch=[
            pltpu.VMEM(block, f32),
            pltpu.VMEM(block, bf16),
            pltpu.SMEM((1,), f32),
            pltpu.SMEM((1,), f32),
            pltpu.SemaphoreType.DMA((3,)),
        ],
    )
    return applied[None, None], alpha, scale


def solution(mesh):
    spec = P(("groups", "sec"), "blk")
    return jax.shard_map(
        shards,
        mesh=mesh,
        in_specs=(spec, spec, spec, spec),
        out_specs=(spec, P(("groups", "sec")), P(("groups", "sec"))),
        check_vma=False,
    )
```

profile of v0, /device:TPU:0, one launch (start us, length us, event | category | flops | bytes accessed | tf_op | source)
XLA Modules:
  0.0 67.4 jit_solution(17880212509194340024)
XLA Ops:
  0.6 0.0 copy-start
  0.6 0.0 copy-start.1
  0.6 2.8 %shard_map.69 = (bf16[14,256,256]{2,1,0:T(8,128)(2,1)}, bf16[1,256,256]{2,1,0:T(8,128)(2,1)S(1)}) custom-call(bf16[17,256,256]{2,1,0:T(8,128)(2,1)} %bitcast.13), custom_call_target="tpu_custom_call" | custom-call | tf_op jit(solution)/shard_map/pallas_call | solution.py:36
  3.5 3.1 %collective-permute-start.2 = (bf16[14,256,256]{2,1,0:T(8,128)(2,1)}, bf16[14,256,256]{2,1,0:T(8,128)(2,1)S(1)}, u32[]{:S(2)}, u32[]{:S(2)}) collective-permute-start(bf16[14,256,256]{2,1,0:T(8,128)(2,1)} %get-tuple-element.29), channel_id=1, source_target_pairs={{0,4},{4,0},{8,12},{12,8},{1,5},{5,1},{9,13},{13,9},{2,6},{6,2},{1... | collective-permute-start | bytes 5505032 | tf_op jit(solution)/shard_map/ppermute | solution.py:24
  6.6 1.0 %shard_map.67 = bf16[2,256,256]{2,1,0:T(8,128)(2,1)S(1)} custom-call(bf16[17,256,256]{2,1,0:T(8,128)(2,1)} %bitcast.14), custom_call_target="tpu_custom_call" | custom-call | tf_op jit(solution)/shard_map/pallas_call | solution.py:36
  7.6 0.1 collective-permute-start
  7.7 2.0 %collective-permute-start.1 = (bf16[1,256,256]{2,1,0:T(8,128)(2,1)S(1)}, bf16[1,256,256]{2,1,0:T(8,128)(2,1)S(1)}, u32[]{:S(2)}, u32[]{:S(2)}) collective-permute-start(bf16[1,256,256]{2,1,0:T(8,128)(2,1)S(1)} %get-tuple-element.28), channel_id=1, source_target_pairs={{0,4},{4,0},{8,12},{12,8},{1,5},{5,1},{9,13},{13,9},{2,6},{6,2},{1... | collective-permute-start | bytes 393224 | tf_op jit(solution)/shard_map/ppermute | solution.py:24
  9.7 0.0 copy-done
  9.7 7.2 %all-gather = bf16[4,1,256,256]{3,2,1,0:T(8,128)(2,1)S(1)} all-gather(bf16[1,1,256,256]{3,2,1,0:T(8,128)(2,1)S(1)} %copy-done), channel_id=2, replica_groups=mesh['groups'=2,'sec'=4,'blk'=4] {'blk'}, dimensions={0}, use_global_device_ids=true | all-gather | bytes 655360 | tf_op jit(solution)/shard_map/all_gather | solution.py:262
  16.8 0.0 copy-done.1
  16.8 0.1 pad_add_fusion.table
  16.9 36.4 %collective-permute-done.chunk = bf16[2,256,256]{2,1,0:T(8,128)(2,1)S(1)} collective-permute-done((bf16[2,256,256]{2,1,0:T(8,128)(2,1)S(1)}, bf16[2,256,256]{2,1,0:T(8,128)(2,1)S(1)}, u32[]{:S(2)}, u32[]{:S(2)}) %collective-permute-start) | collective-permute-done | bytes 262176 | tf_op jit(solution)/shard_map/ppermute | solution.py:24
  53.3 2.7 %shard_map.68 = (bf16[2,17,256,256]{3,2,1,0:T(8,128)(2,1)S(1)}, f32[4,256,256]{2,1,0:T(8,128)S(1)}, f32[4,8,128]{2,1,0:T(8,128)S(1)}, s32[18]{0:T(128)S(4)}, s32[5]{0:T(128)S(4)}, /*index=5*/s32[19]{0:T(128)S(4)}) custom-call(s32[19]{0:T(128)S(1)} %pad_add_fusion.table, bf16[4,256,256]{2,1,0:T(8,128)(2,1)S(1)} %bitcast.7, bf16[17,256,256]{2,1,0:T(8,128)(2,1)} %bitcast.15, ...), custom_call_target="tpu_custom_call" | custom-call | flops 134217728 | tf_op jit(solution)/shard_map/pallas_call | solution.py:36
  56.0 0.0 collective-permute-done.2.chunk
  56.0 1.7 %shard_map.70 = (bf16[2,17,256,256]{3,2,1,0:T(8,128)(2,1)S(1)}, f32[4,256,256]{2,1,0:T(8,128)S(1)}, f32[256,256]{1,0:T(8,128)S(1)}, f32[8,128]{1,0:T(8,128)S(1)}) custom-call(s32[19]{0:T(128)S(4)} %get-tuple-element.25.table, bf16[4,256,256]{2,1,0:T(8,128)(2,1)S(1)} %bitcast.8, ...), custom_call_target="tpu_custom_call", output_to_operand_aliasing={{0}: (3, {}), {1}: (4, {})} | custom-call | flops 939524096 | tf_op jit(solution)/shard_map/pallas_call | solution.py:36
  57.7 0.0 collective-permute-done.1.chunk
  57.7 0.6 shard_map.71
  58.3 2.0 %collective-permute-start.3 = (bf16[264,256]{1,0:T(8,128)(2,1)S(1)}, bf16[264,256]{1,0:T(8,128)(2,1)S(1)}, u32[]{:S(2)}, u32[]{:S(2)}) collective-permute-start(bf16[264,256]{1,0:T(8,128)(2,1)S(1)} %get-tuple-element.38.refs_0_), channel_id=1, source_target_pairs={{0,2},{1,3},{2,0},{3,1},{4,6},{5,7},{6,4},{7,5},{8,10},{9,11},{10,... | collective-permute-start | bytes 405512 | tf_op jit(solution)/shard_map/ppermute | solution.py:24
  60.3 0.0 collective-permute-start.5
  60.3 3.1 %collective-permute-done.3.refs_0_ = bf16[264,256]{1,0:T(8,128)(2,1)S(1)} collective-permute-done((bf16[264,256]{1,0:T(8,128)(2,1)S(1)}, bf16[264,256]{1,0:T(8,128)(2,1)S(1)}, u32[]{:S(2)}, u32[]{:S(2)}) %collective-permute-start.3) | collective-permute-done | bytes 135200 | tf_op jit(solution)/shard_map/ppermute | solution.py:24
  63.4 0.0 collective-permute-start.4
  63.4 0.0 collective-permute-done.5.refs_1_
  63.4 1.7 %shard_map.72 = (f32[256,256]{1,0:T(8,128)S(1)}, f32[2,3,8,128]{3,2,1,0:T(8,128)S(1)}) custom-call(s32[19]{0:T(128)S(4)} %get-tuple-element.25.table, s32[18]{0:T(128)S(4)} %get-tuple-element.26.order, s32[5]{0:T(128)S(4)} %get-tuple-element.27.starts, bf16[4,256,256]{2,1,0:T(8,128)(2,1)S(1)} %bitcast.10, ...), custom_call_target="tpu_custom_call" | custom-call | flops 570425344 | tf_op jit(solution)/shard_map/pallas_call | solution.py:36
  65.1 0.9 %shard_map.73 = (f32[256,256]{1,0:T(8,128)S(1)}, f32[1,3,8,128]{3,2,1,0:T(8,128)S(1)}) custom-call(s32[19]{0:T(128)S(4)} %get-tuple-element.25.table, s32[18]{0:T(128)S(4)} %get-tuple-element.26.order, s32[5]{0:T(128)S(4)} %get-tuple-element.27.starts, bf16[4,256,256]{2,1,0:T(8,128)(2,1)S(1)} %bitcast.11, ...), custom_call_target="tpu_custom_call" | custom-call | flops 285212672 | tf_op jit(solution)/shard_map/pallas_call | solution.py:36
  66.0 0.0 collective-permute-done.4.block
  66.0 1.4 %shard_map.74 = (bf16[256,256]{1,0:T(8,128)(2,1)}, f32[1]{0:T(128)}, f32[1]{0:T(128)}) custom-call(s32[19]{0:T(128)S(4)} %get-tuple-element.25.table, s32[18]{0:T(128)S(4)} %get-tuple-element.26.order, s32[5]{0:T(128)S(4)} %get-tuple-element.27.starts, bf16[4,256,256]{2,1,0:T(8,128)(2,1)S(1)} %bitcast.12, ...), custom_call_target="tpu_custom_call" | custom-call | flops 285212672 | tf_op jit(solution)/shard_map/pallas_call | solution.py:36
Async XLA Ops:
  0.6 9.0 %copy-start = (bf16[1,1,256,256]{3,2,1,0:T(8,128)(2,1)S(1)}, bf16[1,1,256,256]{3,2,1,0:T(8,128)(2,1)}, u32[]{:S(2)}) copy-start(bf16[1,1,256,256]{3,2,1,0:T(8,128)(2,1)} %param.4) | copy-start | bytes 393220
  0.6 16.2 %copy-start.1 = (s32[1,1,17]{2,1,0:T(1,128)S(1)}, s32[1,1,17]{2,1,0:T(1,128)}, u32[]{:S(2)}) copy-start(s32[1,1,17]{2,1,0:T(1,128)} %param.7) | copy-start | bytes 208
  3.5 52.5 %collective-permute-start.2 = (bf16[14,256,256]{2,1,0:T(8,128)(2,1)}, bf16[14,256,256]{2,1,0:T(8,128)(2,1)S(1)}, u32[]{:S(2)}, u32[]{:S(2)}) collective-permute-start(bf16[14,256,256]{2,1,0:T(8,128)(2,1)} %get-tuple-element.29), channel_id=1, source_target_pairs={{0,4},{4,0},{8,12},{12,8},{1,5},{5,1},{9,13},{13,9},{2,6},{6,2},{1... | collective-permute-start | bytes 5505032 | tf_op jit(solution)/shard_map/ppermute | solution.py:24
  7.6 45.7 %collective-permute-start = (bf16[2,256,256]{2,1,0:T(8,128)(2,1)S(1)}, bf16[2,256,256]{2,1,0:T(8,128)(2,1)S(1)}, u32[]{:S(2)}, u32[]{:S(2)}) collective-permute-start(bf16[2,256,256]{2,1,0:T(8,128)(2,1)S(1)} %shard_map.67), channel_id=1, source_target_pairs={{0,4},{4,0},{8,12},{12,8},{1,5},{5,1},{9,13},{13,9},{2,6},{6,2},{1... | collective-permute-start | bytes 786440 | tf_op jit(solution)/shard_map/ppermute | solution.py:24
  7.7 50.0 %collective-permute-start.1 = (bf16[1,256,256]{2,1,0:T(8,128)(2,1)S(1)}, bf16[1,256,256]{2,1,0:T(8,128)(2,1)S(1)}, u32[]{:S(2)}, u32[]{:S(2)}) collective-permute-start(bf16[1,256,256]{2,1,0:T(8,128)(2,1)S(1)} %get-tuple-element.28), channel_id=1, source_target_pairs={{0,4},{4,0},{8,12},{12,8},{1,5},{5,1},{9,13},{13,9},{2,6},{6,2},{1... | collective-permute-start | bytes 393224 | tf_op jit(solution)/shard_map/ppermute | solution.py:24
  58.3 5.1 %collective-permute-start.3 = (bf16[264,256]{1,0:T(8,128)(2,1)S(1)}, bf16[264,256]{1,0:T(8,128)(2,1)S(1)}, u32[]{:S(2)}, u32[]{:S(2)}) collective-permute-start(bf16[264,256]{1,0:T(8,128)(2,1)S(1)} %get-tuple-element.38.refs_0_), channel_id=1, source_target_pairs={{0,2},{1,3},{2,0},{3,1},{4,6},{5,7},{6,4},{7,5},{8,10},{9,11},{10,... | collective-permute-start | bytes 405512 | tf_op jit(solution)/shard_map/ppermute | solution.py:24
  60.3 3.1 %collective-permute-start.5 = (bf16[264,256]{1,0:T(8,128)(2,1)S(1)}, bf16[264,256]{1,0:T(8,128)(2,1)S(1)}, u32[]{:S(2)}, u32[]{:S(2)}) collective-permute-start(bf16[264,256]{1,0:T(8,128)(2,1)S(1)} %get-tuple-element.38.refs_0_), channel_id=1, source_target_pairs={{0,1},{1,0},{2,3},{3,2},{4,5},{5,4},{6,7},{7,6},{8,9},{9,8},{10,11... | collective-permute-start | bytes 405512 | tf_op jit(solution)/shard_map/ppermute | solution.py:24
  63.4 2.6 %collective-permute-start.4 = (bf16[264,256]{1,0:T(8,128)(2,1)S(1)}, bf16[264,256]{1,0:T(8,128)(2,1)S(1)}, u32[]{:S(2)}, u32[]{:S(2)}) collective-permute-start(bf16[264,256]{1,0:T(8,128)(2,1)S(1)} %collective-permute-done.3.refs_0_), channel_id=1, source_target_pairs={{0,1},{1,0},{2,3},{3,2},{4,5},{5,4},{6,7},{7,6},{8,9},{9,8},{10,11... | collective-permute-start | bytes 405512 | tf_op jit(solution)/shard_map/ppermute | solution.py:24
where the time goes:
time: 67.6 us; the launch traced here: 67.4 us
  waiting for transfers between devices  39.5 us (58%)
  Pallas kernels  12.7 us (19%)
  starting transfers between devices  7.21 us (11%)
  blocking collectives  7.16 us (11%)
  between operations  0.73 us (1%)
    ppermute x6, waiting for transfers between devices, swap(): lax.ppermute(value, axis, [(i, i ^ bit) for i in range(lax.axis_size(axis...  39.5 us
    pallas_call x8, Pallas kernels, call(): pl.pallas_call(kernel, in_specs=ins, out_specs=[spec for spec, _ in outs]...  12.7 us
    ppermute x6, starting transfers between devices, swap(): lax.ppermute(value, axis, [(i, i ^ bit) for i in range(lax.axis_size(axis...  7.21 us
    all_gather x1, blocking collectives, shards(): psis = lax.all_gather(psi[0, 0], 'blk', axis=0)  7.16 us
  transfers between devices with their start and end apart: 6, of which 2 were waited for; matrix products, arithmetic and copies ran while one was open for 0% of the time, Pallas kernels for 12%

commit v1 on v0

--- a/solution.py
+++ b/solution.py
@@ -144,7 +144,8 @@
         else:
             vector = blocks[0][:psi_rows]
         inner = dot(vector, env[1 - parity, c])
-        inners.append(jnp.where(valid, inner, 0.0).astype(bf16))
+        rounded = inner.astype(bf16)
+        inners.append(jnp.where(valid, rounded, jnp.zeros_like(rounded)))
         lefts.append(env[parity, c])
     return dot(jnp.concatenate(lefts, axis=1), jnp.concatenate(inners, axis=0))
 
@@ -304,7 +305,7 @@
             blocks[m | bit] = swap(blocks[m], "blk", bit)
         bit //= 2
 
-    cuts = sorted({0, min(2, width - 1), width - 1})
+    cuts = sorted({0, min(1, width - 1), min(2, width - 1), width - 1})
     shared = [table, order, starts, psis, env]
     shared_specs = [SMEM, SMEM, SMEM, VMEM, VMEM]
     summed, stats = None, []

time: 67.6 us -> 67.8 us (level)
    pallas_call x8 -> x9, Pallas kernels: 12.7 us -> 12.9 us  [call(): pl.pallas_call(kernel, in_specs=ins, out_specs=[spec for spec, _ in outs]...]
where the time goes in v1:
time: 67.8 us; the launch traced here: 67.5 us
  waiting for transfers between devices  39.5 us (58%)
  Pallas kernels  12.9 us (19%)
  starting transfers between devices  7.21 us (11%)
  blocking collectives  7.16 us (11%)
  between operations  0.74 us (1%)
    ppermute x6, waiting for transfers between devices, swap(): lax.ppermute(value, axis, [(i, i ^ bit) for i in range(lax.axis_size(axis...  39.5 us
    pallas_call x9, Pallas kernels, call(): pl.pallas_call(kernel, in_specs=ins, out_specs=[spec for spec, _ in outs]...  12.9 us
    ppermute x6, starting transfers between devices, swap(): lax.ppermute(value, axis, [(i, i ^ bit) for i in range(lax.axis_size(axis...  7.21 us
    all_gather x1, blocking collectives, shards(): psis = lax.all_gather(psi[0, 0], 'blk', axis=0)  7.16 us
  transfers between devices with their start and end apart: 6, of which 2 were waited for; matrix products, arithmetic and copies ran while one was open for 0% of the time, Pallas kernels for 12%

profile of v1, /device:TPU:0, one launch (start us, length us, event | category | flops | bytes accessed | tf_op | source)
XLA Modules:
  0.0 67.5 jit_solution(16461149439168063091)
XLA Ops:
  0.6 0.0 copy-start
  0.6 0.0 copy-start.1
  0.6 2.8 %shard_map.69 = (bf16[14,256,256]{2,1,0:T(8,128)(2,1)}, bf16[1,256,256]{2,1,0:T(8,128)(2,1)S(1)}) custom-call(bf16[17,256,256]{2,1,0:T(8,128)(2,1)} %bitcast.14), custom_call_target="tpu_custom_call" | custom-call | tf_op jit(solution)/shard_map/pallas_call | solution.py:36
  3.5 3.1 %collective-permute-start.2 = (bf16[14,256,256]{2,1,0:T(8,128)(2,1)}, bf16[14,256,256]{2,1,0:T(8,128)(2,1)S(1)}, u32[]{:S(2)}, u32[]{:S(2)}) collective-permute-start(bf16[14,256,256]{2,1,0:T(8,128)(2,1)} %get-tuple-element.31), channel_id=1, source_target_pairs={{0,4},{4,0},{8,12},{12,8},{1,5},{5,1},{9,13},{13,9},{2,6},{6,2},{1... | collective-permute-start | bytes 5505032 | tf_op jit(solution)/shard_map/ppermute | solution.py:24
  6.6 1.0 %shard_map.67 = bf16[2,256,256]{2,1,0:T(8,128)(2,1)S(1)} custom-call(bf16[17,256,256]{2,1,0:T(8,128)(2,1)} %bitcast.15), custom_call_target="tpu_custom_call" | custom-call | tf_op jit(solution)/shard_map/pallas_call | solution.py:36
  7.6 0.1 collective-permute-start
  7.7 2.0 %collective-permute-start.1 = (bf16[1,256,256]{2,1,0:T(8,128)(2,1)S(1)}, bf16[1,256,256]{2,1,0:T(8,128)(2,1)S(1)}, u32[]{:S(2)}, u32[]{:S(2)}) collective-permute-start(bf16[1,256,256]{2,1,0:T(8,128)(2,1)S(1)} %get-tuple-element.30), channel_id=1, source_target_pairs={{0,4},{4,0},{8,12},{12,8},{1,5},{5,1},{9,13},{13,9},{2,6},{6,2},{1... | collective-permute-start | bytes 393224 | tf_op jit(solution)/shard_map/ppermute | solution.py:24
  9.7 0.0 copy-done
  9.7 7.2 %all-gather = bf16[4,1,256,256]{3,2,1,0:T(8,128)(2,1)S(1)} all-gather(bf16[1,1,256,256]{3,2,1,0:T(8,128)(2,1)S(1)} %copy-done), channel_id=2, replica_groups=mesh['groups'=2,'sec'=4,'blk'=4] {'blk'}, dimensions={0}, use_global_device_ids=true | all-gather | bytes 655360 | tf_op jit(solution)/shard_map/all_gather | solution.py:263
  16.8 0.0 copy-done.1
  16.8 0.1 pad_add_fusion.table
  16.9 36.4 %collective-permute-done.chunk = bf16[2,256,256]{2,1,0:T(8,128)(2,1)S(1)} collective-permute-done((bf16[2,256,256]{2,1,0:T(8,128)(2,1)S(1)}, bf16[2,256,256]{2,1,0:T(8,128)(2,1)S(1)}, u32[]{:S(2)}, u32[]{:S(2)}) %collective-permute-start) | collective-permute-done | bytes 262176 | tf_op jit(solution)/shard_map/ppermute | solution.py:24
  53.3 2.7 %shard_map.68 = (bf16[2,17,256,256]{3,2,1,0:T(8,128)(2,1)S(1)}, f32[4,256,256]{2,1,0:T(8,128)S(1)}, f32[4,8,128]{2,1,0:T(8,128)S(1)}, s32[18]{0:T(128)S(4)}, s32[5]{0:T(128)S(4)}, /*index=5*/s32[19]{0:T(128)S(4)}) custom-call(s32[19]{0:T(128)S(1)} %pad_add_fusion.table, bf16[4,256,256]{2,1,0:T(8,128)(2,1)S(1)} %bitcast.7, bf16[17,256,256]{2,1,0:T(8,128)(2,1)} %bitcast.16, ...), custom_call_target="tpu_custom_call" | custom-call | flops 134217728 | tf_op jit(solution)/shard_map/pallas_call | solution.py:36
  56.0 0.0 collective-permute-done.2.chunk
  56.0 1.7 %shard_map.70 = (bf16[2,17,256,256]{3,2,1,0:T(8,128)(2,1)S(1)}, f32[4,256,256]{2,1,0:T(8,128)S(1)}, f32[256,256]{1,0:T(8,128)S(1)}, f32[8,128]{1,0:T(8,128)S(1)}) custom-call(s32[19]{0:T(128)S(4)} %get-tuple-element.27.table, bf16[4,256,256]{2,1,0:T(8,128)(2,1)S(1)} %bitcast.8, ...), custom_call_target="tpu_custom_call", output_to_operand_aliasing={{0}: (3, {}), {1}: (4, {})} | custom-call | flops 939524096 | tf_op jit(solution)/shard_map/pallas_call | solution.py:36
  57.7 0.0 collective-permute-done.1.chunk
  57.7 0.6 shard_map.71
  58.3 2.0 %collective-permute-start.3 = (bf16[264,256]{1,0:T(8,128)(2,1)S(1)}, bf16[264,256]{1,0:T(8,128)(2,1)S(1)}, u32[]{:S(2)}, u32[]{:S(2)}) collective-permute-start(bf16[264,256]{1,0:T(8,128)(2,1)S(1)} %get-tuple-element.40.refs_0_), channel_id=1, source_target_pairs={{0,2},{1,3},{2,0},{3,1},{4,6},{5,7},{6,4},{7,5},{8,10},{9,11},{10,... | collective-permute-start | bytes 405512 | tf_op jit(solution)/shard_map/ppermute | solution.py:24
  60.3 0.0 collective-permute-start.5
  60.3 3.1 %collective-permute-done.3.refs_0_ = bf16[264,256]{1,0:T(8,128)(2,1)S(1)} collective-permute-done((bf16[264,256]{1,0:T(8,128)(2,1)S(1)}, bf16[264,256]{1,0:T(8,128)(2,1)S(1)}, u32[]{:S(2)}, u32[]{:S(2)}) %collective-permute-start.3) | collective-permute-done | bytes 135200 | tf_op jit(solution)/shard_map/ppermute | solution.py:24
  63.4 0.0 collective-permute-start.4
  63.4 0.9 %shard_map.72 = (f32[256,256]{1,0:T(8,128)S(1)}, f32[1,3,8,128]{3,2,1,0:T(8,128)S(1)}) custom-call(s32[19]{0:T(128)S(4)} %get-tuple-element.27.table, s32[18]{0:T(128)S(4)} %get-tuple-element.28.order, s32[5]{0:T(128)S(4)} %get-tuple-element.29.starts, bf16[4,256,256]{2,1,0:T(8,128)(2,1)S(1)} %bitcast.10, ...), custom_call_target="tpu_custom_call" | custom-call | flops 285212672 | tf_op jit(solution)/shard_map/pallas_call | solution.py:36
  64.3 0.0 collective-permute-done.5.refs_0_
  64.3 0.9 %shard_map.73 = (f32[256,256]{1,0:T(8,128)S(1)}, f32[1,3,8,128]{3,2,1,0:T(8,128)S(1)}) custom-call(s32[19]{0:T(128)S(4)} %get-tuple-element.27.table, s32[18]{0:T(128)S(4)} %get-tuple-element.28.order, s32[5]{0:T(128)S(4)} %get-tuple-element.29.starts, bf16[4,256,256]{2,1,0:T(8,128)(2,1)S(1)} %bitcast.11, ...), custom_call_target="tpu_custom_call" | custom-call | flops 285212672 | tf_op jit(solution)/shard_map/pallas_call | solution.py:36
  65.2 0.9 %shard_map.74 = (f32[256,256]{1,0:T(8,128)S(1)}, f32[1,3,8,128]{3,2,1,0:T(8,128)S(1)}) custom-call(s32[19]{0:T(128)S(4)} %get-tuple-element.27.table, s32[18]{0:T(128)S(4)} %get-tuple-element.28.order, s32[5]{0:T(128)S(4)} %get-tuple-element.29.starts, bf16[4,256,256]{2,1,0:T(8,128)(2,1)S(1)} %bitcast.12, ...), custom_call_target="tpu_custom_call" | custom-call | flops 285212672 | tf_op jit(solution)/shard_map/pallas_call | solution.py:36
  66.1 0.0 collective-permute-done.4.block
  66.1 1.4 %shard_map.75 = (bf16[256,256]{1,0:T(8,128)(2,1)}, f32[1]{0:T(128)}, f32[1]{0:T(128)}) custom-call(s32[19]{0:T(128)S(4)} %get-tuple-element.27.table, s32[18]{0:T(128)S(4)} %get-tuple-element.28.order, s32[5]{0:T(128)S(4)} %get-tuple-element.29.starts, bf16[4,256,256]{2,1,0:T(8,128)(2,1)S(1)} %bitcast.13, ...), custom_call_target="tpu_custom_call" | custom-call | flops 285212672 | tf_op jit(solution)/shard_map/pallas_call | solution.py:36
Async XLA Ops:
  0.6 9.0 %copy-start = (bf16[1,1,256,256]{3,2,1,0:T(8,128)(2,1)S(1)}, bf16[1,1,256,256]{3,2,1,0:T(8,128)(2,1)}, u32[]{:S(2)}) copy-start(bf16[1,1,256,256]{3,2,1,0:T(8,128)(2,1)} %param.4) | copy-start | bytes 393220
  0.6 16.2 %copy-start.1 = (s32[1,1,17]{2,1,0:T(1,128)S(1)}, s32[1,1,17]{2,1,0:T(1,128)}, u32[]{:S(2)}) copy-start(s32[1,1,17]{2,1,0:T(1,128)} %param.7) | copy-start | bytes 208
  3.5 52.5 %collective-permute-start.2 = (bf16[14,256,256]{2,1,0:T(8,128)(2,1)}, bf16[14,256,256]{2,1,0:T(8,128)(2,1)S(1)}, u32[]{:S(2)}, u32[]{:S(2)}) collective-permute-start(bf16[14,256,256]{2,1,0:T(8,128)(2,1)} %get-tuple-element.31), channel_id=1, source_target_pairs={{0,4},{4,0},{8,12},{12,8},{1,5},{5,1},{9,13},{13,9},{2,6},{6,2},{1... | collective-permute-start | bytes 5505032 | tf_op jit(solution)/shard_map/ppermute | solution.py:24
  7.6 45.7 %collective-permute-start = (bf16[2,256,256]{2,1,0:T(8,128)(2,1)S(1)}, bf16[2,256,256]{2,1,0:T(8,128)(2,1)S(1)}, u32[]{:S(2)}, u32[]{:S(2)}) collective-permute-start(bf16[2,256,256]{2,1,0:T(8,128)(2,1)S(1)} %shard_map.67), channel_id=1, source_target_pairs={{0,4},{4,0},{8,12},{12,8},{1,5},{5,1},{9,13},{13,9},{2,6},{6,2},{1... | collective-permute-start | bytes 786440 | tf_op jit(solution)/shard_map/ppermute | solution.py:24
  7.7 50.0 %collective-permute-start.1 = (bf16[1,256,256]{2,1,0:T(8,128)(2,1)S(1)}, bf16[1,256,256]{2,1,0:T(8,128)(2,1)S(1)}, u32[]{:S(2)}, u32[]{:S(2)}) collective-permute-start(bf16[1,256,256]{2,1,0:T(8,128)(2,1)S(1)} %get-tuple-element.30), channel_id=1, source_target_pairs={{0,4},{4,0},{8,12},{12,8},{1,5},{5,1},{9,13},{13,9},{2,6},{6,2},{1... | collective-permute-start | bytes 393224 | tf_op jit(solution)/shard_map/ppermute | solution.py:24
  58.3 5.1 %collective-permute-start.3 = (bf16[264,256]{1,0:T(8,128)(2,1)S(1)}, bf16[264,256]{1,0:T(8,128)(2,1)S(1)}, u32[]{:S(2)}, u32[]{:S(2)}) collective-permute-start(bf16[264,256]{1,0:T(8,128)(2,1)S(1)} %get-tuple-element.40.refs_0_), channel_id=1, source_target_pairs={{0,2},{1,3},{2,0},{3,1},{4,6},{5,7},{6,4},{7,5},{8,10},{9,11},{10,... | collective-permute-start | bytes 405512 | tf_op jit(solution)/shard_map/ppermute | solution.py:24
  60.3 4.0 %collective-permute-start.5 = (bf16[264,256]{1,0:T(8,128)(2,1)S(1)}, bf16[264,256]{1,0:T(8,128)(2,1)S(1)}, u32[]{:S(2)}, u32[]{:S(2)}) collective-permute-start(bf16[264,256]{1,0:T(8,128)(2,1)S(1)} %get-tuple-element.40.refs_0_), channel_id=1, source_target_pairs={{0,1},{1,0},{2,3},{3,2},{4,5},{5,4},{6,7},{7,6},{8,9},{9,8},{10,11... | collective-permute-start | bytes 405512 | tf_op jit(solution)/shard_map/ppermute | solution.py:24
  63.4 2.8 %collective-permute-start.4 = (bf16[264,256]{1,0:T(8,128)(2,1)S(1)}, bf16[264,256]{1,0:T(8,128)(2,1)S(1)}, u32[]{:S(2)}, u32[]{:S(2)}) collective-permute-start(bf16[264,256]{1,0:T(8,128)(2,1)S(1)} %collective-permute-done.3.refs_0_), channel_id=1, source_target_pairs={{0,1},{1,0},{2,3},{3,2},{4,5},{5,4},{6,7},{7,6},{8,9},{9,8},{10,11... | collective-permute-start | bytes 405512 | tf_op jit(solution)/shard_map/ppermute | solution.py:24
